TPU v7x, 32 devices: a whole 2x2x4 slice. The times are simulated.
32 devices in a mesh: py: 4 (over y, x), pz: 8 (over z, core).
Axes of the slice: x: 2, y: 2, z: 4, core: 2. Of those that a mesh axis runs over, the one named last changes fastest.
Arguments:
- species: float32 [4, 512, 64, 64], P(None, None, 'py', 'pz'), may hold values from -6 to 6
- coupling: float32 [4, 4], replicated, may hold values from -4 to 4
- symbol_x: float32 [512], replicated, may hold values from 0.3 to 3
- symbol_y: float32 [64], replicated, may hold values from 0.3 to 3
- symbol_z: float32 [64], replicated, may hold values from 0.3 to 3
Outputs:
- modes: float32 [4, 512, 64, 64], P(None, 'py', 'pz')
All inputs are finite; a program needn't handle non-finite values.
Results may differ from a plain program's by a relative error of at most 0.00007.
Values sent between devices are 32-bit elements; how exact they have to be, the bound alone decides.
A program may use at most 64 MiB of HBM per device.

v0:
```python
import jax
import jax.numpy as jnp
from jax import lax
from jax.sharding import PartitionSpec as P


def mode_table(count):
    rank = jnp.arange(count)
    angle = (
        jnp.pi
        / (4 * count)
        * ((2 * rank[:, None] + 1) * (2 * rank[None, :] + 1) % (8 * count)).astype(jnp.float32)
    )
    return jnp.cos(angle) * (2.0 / count) ** 0.5


def transform_dim(values, dim):
    moved = jnp.tensordot(
        values, mode_table(values.shape[dim]), axes=([dim], [0]), precision=lax.Precision.HIGHEST
    )
    return jnp.moveaxis(moved, -1, dim)


def shards(species, coupling, symbol_x, symbol_y, symbol_z):
    part_values = species
    part_values = transform_dim(part_values, 1)
    part_values = lax.all_to_all(part_values, "py", split_axis=1, concat_axis=2, tiled=True)
    part_values = transform_dim(part_values, 2)
    pencil_values = part_values
    pencil_values = lax.all_to_all(pencil_values, "pz", split_axis=2, concat_axis=3, tiled=True)
    pencil_values = transform_dim(pencil_values, 3)
    share_x = pencil_values.shape[1]
    part_x = lax.dynamic_slice_in_dim(symbol_x, lax.axis_index("py") * share_x, share_x)
    share_y = pencil_values.shape[2]
    part_y = lax.dynamic_slice_in_dim(symbol_y, lax.axis_index("pz") * share_y, share_y)
    symbol = part_x[:, None, None] + part_y[None, :, None] + symbol_z[None, None, :]
    weight_xyz = 1.0 / (1.0 + symbol)
    mixed_fields = jnp.einsum(
        "ab,bxyz->axyz", coupling, pencil_values, precision=lax.Precision.HIGHEST
    )
    pencil_values = weight_xyz * pencil_values + (1.0 - weight_xyz) * mixed_fields
    return pencil_values


def solution(mesh):
    return jax.shard_map(
        shards,
        mesh=mesh,
        in_specs=(P(None, None, "py", "pz"), P(), P(), P(), P()),
        out_specs=P(None, "py", "pz", None),
        check_vma=False,
    )
```

profile of v0, /device:TPU:0, one launch (start us, length us, event | category | flops | bytes accessed | tf_op | source)
XLA Modules:
  0.0 95.0 jit_solution(6037659753878143256)
XLA Ops:
  0.0 0.0 copy-start
  0.0 1.2 %copy-done = f32[4,512,16,8]{1,3,2,0:T(8,128)S(1)} copy-done((f32[4,512,16,8]{1,3,2,0:T(8,128)S(1)}, f32[4,512,16,8]{1,3,2,0:T(8,128)}, u32[]{:S(2)}) %copy-start) | copy-done | bytes 1048600
  1.2 6.2 %convolution_bitcast_fusion.1 = f32[4,512,16,8]{1,2,3,0:T(8,128)S(1)} fusion(f32[4,512,16,8]{1,3,2,0:T(8,128)S(1)} %copy-done, s32[512]{0:T(512)S(1)} %multiply_add_fusion), kind=kOutput, calls=%fused_computation.6 | convolution fusion | flops 1614544896 | bytes 2099200 | tf_op jit(solution)/shard_map/dot_general | solution.py:18
  7.4 7.5 %copy.12 = f32[4,512,16,8]{2,3,0,1:T(8,128)} copy(f32[4,512,16,8]{1,2,3,0:T(8,128)S(1)} %convolution_bitcast_fusion.1) | data formatting | bytes 2097152 | tf_op jit(solution)/shard_map/transpose | solution.py:21
  14.9 6.4 %reshape.68 = f32[4,1,65536]{2,1,0:T(1,128)} reshape(f32[512,4,8,16]{3,2,1,0:T(8,128)} %bitcast.35) | data formatting | bytes 2097152
  21.3 5.2 %all-to-all-start = ((f32[4,1,65536]{2,1,0:T(1,128)}), f32[4,1,65536]{2,1,0:T(1,128)S(1)}, u32[]{:S(2)}, u32[]{:S(2)}) async-start(f32[4,1,65536]{2,1,0:T(1,128)} %reshape.68), calls=%async_computation | async-start | bytes 2097152 | tf_op jit(solution)/shard_map/all_to_all | solution.py:27
  26.5 13.6 %all-to-all-done = f32[4,1,65536]{2,1,0:T(1,128)S(1)} async-done(((f32[4,1,65536]{2,1,0:T(1,128)}), f32[4,1,65536]{2,1,0:T(1,128)S(1)}, u32[]{:S(2)}, u32[]{:S(2)}) %all-to-all-start) | async-done | bytes 1048608 | tf_op jit(solution)/shard_map/all_to_all | solution.py:27
  40.1 0.5 broadcast.168
  40.6 3.7 %reduce = f32[4,65536]{1,0:T(4,128)S(1)} reduce(f32[4,1,65536]{2,1,0:T(1,128)S(1)} %all-to-all-done, f32[]{:T(128)} %broadcast.168), dimensions={1}, to_apply=%all_to_all.26.reduce_sub_computation | reduce | bytes 2097156 | tf_op jit(solution)/shard_map/all_to_all | solution.py:27
  44.3 6.1 %reshape.69 = f32[512,4,8,16]{3,2,1,0:T(8,128)} reshape(f32[4,65536]{1,0:T(4,128)S(1)} %reduce) | data formatting | bytes 2097152
  50.5 0.0 copy-start.3
  50.5 0.0 copy-start.2
  50.5 0.0 copy-start.1
  50.5 5.2 %copy.13 = f32[4,4,128,16,8]{2,3,1,4,0:T(8,128)S(1)} copy(f32[4,4,128,16,8]{3,4,0,2,1:T(8,128)} %bitcast.36) | data formatting | bytes 2097152 | tf_op jit(solution)/shard_map/all_to_all | solution.py:27
  55.6 1.3 %convolution_bitcast_fusion = f32[4,128,64,8]{1,2,3,0:T(8,128)S(1)} fusion(f32[4,128,64,8]{1,2,3,0:T(8,128)S(1)} %bitcast.37, s32[64]{0:T(128)S(1)} %multiply_add_fusion.1), kind=kOutput, calls=%fused_computation.5 | convolution fusion | flops 201388032 | bytes 2097408 | tf_op jit(solution)/shard_map/dot_general | solution.py:18
  56.9 1.6 %copy.14 = f32[4,128,64,8]{1,3,0,2:T(8,128)} copy(f32[4,128,64,8]{1,2,3,0:T(8,128)S(1)} %convolution_bitcast_fusion) | data formatting | bytes 2097152 | tf_op jit(solution)/shard_map/transpose | solution.py:21
  58.5 4.9 %all-to-all-start.1 = ((f32[4,128,64,8]{1,3,0,2:T(8,128)}), f32[4,128,64,8]{1,3,0,2:T(8,128)S(1)}, u32[]{:S(2)}, u32[]{:S(2)}) async-start(f32[4,128,64,8]{1,3,0,2:T(8,128)} %copy.14), calls=%async_computation.1 | async-start | bytes 2097152 | tf_op jit(solution)/shard_map/all_to_all | solution.py:30
  63.4 0.0 copy-done.3
  63.4 0.1 dynamic_slice.7
  63.5 0.8 dynamic_slice.6
  64.3 0.1 broadcast_add_fusion
  64.4 0.0 copy-done.2
  64.4 0.1 add_divide_fusion
  64.5 25.5 %all-to-all-done.1 = f32[4,128,64,8]{1,3,0,2:T(8,128)S(1)} async-done(((f32[4,128,64,8]{1,3,0,2:T(8,128)}), f32[4,128,64,8]{1,3,0,2:T(8,128)S(1)}, u32[]{:S(2)}, u32[]{:S(2)}) %all-to-all-start.1) | async-done | bytes 1048608 | tf_op jit(solution)/shard_map/all_to_all | solution.py:30
  90.0 1.3 %fusion.7 = f32[4,128,8,64]{1,3,2,0:T(8,128)S(1)} fusion(f32[4,128,8,8,8]{1,4,0,3,2:T(8,128)S(1)} %bitcast.38, s32[64]{0:T(128)S(1)} %multiply_add_fusion.1), kind=kOutput, calls=%fused_computation.13 | convolution fusion | flops 201388032 | bytes 2097408 | tf_op jit(solution)/shard_map/dot_general | solution.py:18
  91.3 0.0 copy-done.1
  91.3 2.5 %fusion.9 = f32[128,8,64,4]{0,3,2,1:T(4,128)S(1)} fusion(f32[4,128,8,64]{1,3,2,0:T(8,128)S(1)} %fusion.7, f32[4,4]{1,0:T(4,128)S(1)} %copy-done.1), kind=kOutput, calls=%fused_computation.17 | convolution fusion | flops 12582912 | bytes 2097216 | tf_op jit(solution)/shard_map/ab,bxyz->axyz/dot_general | solution.py:38
  93.8 1.2 %bitcast_add_fusion = f32[4,128,8,64]{1,3,2,0:T(8,128)} fusion(f32[128,8,64,4]{0,3,2,1:T(4,128)S(1)} %fusion.9, f32[4,128,8,64]{1,3,2,0:T(8,128)S(1)} %fusion.7, f32[128,8,64]{0,2,1:T(8,128)S(1)} %get-tuple-element.6, f32[128,8,64]{0,2,1:T(8,128)S(1)} %get-tuple-element.5), kind=kLoop, calls=%fused_computation.15 | loop fusion | flops 786432 | bytes 3670016 | tf_op jit(solution)/shard_map/add | solution.py:41
  (2 shorter events, 0.0 us)
Async XLA Ops:
  0.0 1.2 %copy-start = (f32[4,512,16,8]{1,3,2,0:T(8,128)S(1)}, f32[4,512,16,8]{1,3,2,0:T(8,128)}, u32[]{:S(2)}) copy-start(f32[4,512,16,8]{1,3,2,0:T(8,128)} %param.5) | copy-start | bytes 3145732
  21.3 18.8 %all-to-all-start = ((f32[4,1,65536]{2,1,0:T(1,128)}), f32[4,1,65536]{2,1,0:T(1,128)S(1)}, u32[]{:S(2)}, u32[]{:S(2)}) async-start(f32[4,1,65536]{2,1,0:T(1,128)} %reshape.68), calls=%async_computation | async-start | bytes 2097152 | tf_op jit(solution)/shard_map/all_to_all | solution.py:27
  50.5 13.0 %copy-start.3 = (f32[64]{0:T(128)S(1)}, f32[64]{0:T(128)}, u32[]{:S(2)}) copy-start(f32[64]{0:T(128)} %param.8) | copy-start | bytes 772
  50.5 13.9 %copy-start.2 = (f32[64]{0:T(128)S(1)}, f32[64]{0:T(128)}, u32[]{:S(2)}) copy-start(f32[64]{0:T(128)} %param.9) | copy-start | bytes 772
  50.5 40.8 %copy-start.1 = (f32[4,4]{1,0:T(4,128)S(1)}, f32[4,4]{1,0:T(4,128)}, u32[]{:S(2)}) copy-start(f32[4,4]{1,0:T(4,128)} %param.6) | copy-start | bytes 196
  58.5 31.5 %all-to-all-start.1 = ((f32[4,128,64,8]{1,3,0,2:T(8,128)}), f32[4,128,64,8]{1,3,0,2:T(8,128)S(1)}, u32[]{:S(2)}, u32[]{:S(2)}) async-start(f32[4,128,64,8]{1,3,0,2:T(8,128)} %copy.14), calls=%async_computation.1 | async-start | bytes 2097152 | tf_op jit(solution)/shard_map/all_to_all | solution.py:30
where the time goes:
time: 95.4 us; the launch traced here: 95 us
  waiting for transfers between devices  39.1 us (41%)
  local copies, waits for them, and re-layouts  29.3 us (31%)
  matrix products  11.2 us (12%)
  starting transfers between devices  10.1 us (11%)
  other arithmetic  5.07 us (5%)
    all_to_all x1, waiting for transfers between devices, shards(): lax.all_to_all(pencil_values, 'pz', split_axis=2, concat_axis=3, tiled=True)  25.5 us
    unnamed x10, local copies, waits for them, and re-layouts  13.8 us
    all_to_all x1, waiting for transfers between devices, shards(): lax.all_to_all(part_values, 'py', split_axis=1, concat_axis=2, tiled=True)  13.6 us
    transpose x2, local copies, waits for them, and re-layouts, transform_dim(): return jnp.moveaxis(moved, -1, dim)  9.07 us
    dot_general x3, matrix products, transform_dim(): jnp.tensordot(values, mode_table(values.shape[dim]), axes=([dim], [0]), p...  8.73 us
    all_to_all x2, local copies, waits for them, and re-layouts, shards(): lax.all_to_all(part_values, 'py', split_axis=1, concat_axis=2, tiled=True)  5.68 us
    all_to_all x1, starting transfers between devices, shards(): lax.all_to_all(part_values, 'py', split_axis=1, concat_axis=2, tiled=True)  5.19 us
    all_to_all x1, starting transfers between devices, shards(): lax.all_to_all(pencil_values, 'pz', split_axis=2, concat_axis=3, tiled=True)  4.93 us
  transfers between devices with their start and end apart: 2, of which 2 were waited for; matrix products, arithmetic and copies ran while one was open for 1% of the time, Pallas kernels for 0%

commit v1 on v0

v1 whole, which is shorter than its diff:
```python
import functools

import jax
import jax.numpy as jnp
import numpy as np
from jax import lax
from jax.experimental import pallas as pl
from jax.experimental.pallas import tpu as pltpu
from jax.sharding import PartitionSpec as P

MESH = pl.DeviceIdType.MESH
F32 = jnp.float32
BF16 = jnp.bfloat16
LANES, SUBLANES = 128, 8
VMEM_BUDGET = 48 << 20


def mode_table(count):
    rank = jnp.arange(count)
    angle = (
        jnp.pi
        / (4 * count)
        * ((2 * rank[:, None] + 1) * (2 * rank[None, :] + 1) % (8 * count)).astype(jnp.float32)
    )
    return jnp.cos(angle) * (2.0 / count) ** 0.5


def transform_dim(values, dim):
    moved = jnp.tensordot(
        values, mode_table(values.shape[dim]), axes=([dim], [0]), precision=lax.Precision.HIGHEST
    )
    return jnp.moveaxis(moved, -1, dim)


def plain_shards(species, coupling, symbol_x, symbol_y, symbol_z):
    values = transform_dim(species, 1)
    values = lax.all_to_all(values, "py", split_axis=1, concat_axis=2, tiled=True)
    values = transform_dim(values, 2)
    values = lax.all_to_all(values, "pz", split_axis=2, concat_axis=3, tiled=True)
    values = transform_dim(values, 3)
    share_x = values.shape[1]
    part_x = lax.dynamic_slice_in_dim(symbol_x, lax.axis_index("py") * share_x, share_x)
    share_y = values.shape[2]
    part_y = lax.dynamic_slice_in_dim(symbol_y, lax.axis_index("pz") * share_y, share_y)
    symbol = part_x[:, None, None] + part_y[None, :, None] + symbol_z[None, None, :]
    weight = 1.0 / (1.0 + symbol)
    mixed = jnp.einsum("ab,bxyz->axyz", coupling, values, precision=lax.Precision.HIGHEST)
    return weight * values + (1.0 - weight) * mixed


def split_table(count):
    rank = 2 * np.arange(count) + 1
    table = np.cos(np.pi / (4 * count) * (rank[:, None] * rank[None, :] % (8 * count)))
    table = (table * np.sqrt(2.0 / count)).astype(np.float32)
    high = table.astype(BF16)
    low = (table - high.astype(np.float32)).astype(BF16)
    return np.stack([high, low])


def split(values):
    high = values.astype(BF16)
    low = (values - high.astype(F32)).astype(BF16)
    return high, low


def dot(a, b):
    return jnp.dot(a, b, preferred_element_type=F32)


def flipped(index, offset, count):
    if count & (count - 1):
        return lax.rem(index + offset, count)
    result = index
    bit = 1
    while bit < count:
        if offset & bit:
            result = result + bit - 2 * bit * lax.rem(index // bit, 2)
        bit *= 2
    return result


def source_of(index, offset, count):
    if count & (count - 1):
        return lax.rem(index + count - offset, count)
    return flipped(index, offset, count)


def kernel(
    dims, field_ref, hx_hbm, hy_ref, hz_ref, coupling_ref, sx_ref, sy_ref, sz_ref, out_ref,
    held, hx, lines_out, lines, parts_out, parts, modes, my, mz,
    load_sem, hx_sem, send_y, recv_y, send_z, recv_z,
):
    fields, ny, nz, n_py, n_pz, yl, zl, share_x, share_y = dims
    py, pz = lax.axis_index("py"), lax.axis_index("pz")
    rows_y = yl * zl
    rows_z = share_y * zl
    depth_y = ny * zl
    rows_out = share_y * nz
    depth_z = n_pz * rows_z

    def load(f):
        return pltpu.make_async_copy(field_ref.at[f], held.at[f], load_sem.at[f])

    hx_copy = pltpu.make_async_copy(hx_hbm, hx, hx_sem)
    load(0).start()
    hx_copy.start()
    for f in range(1, fields):
        load(f).start()
    barrier = pltpu.get_barrier_semaphore()
    for o in range(1, n_pz):
        pl.semaphore_signal(
            barrier, inc=1, device_id={"pz": flipped(pz, o, n_pz)}, device_id_type=MESH
        )
    for o in range(1, n_py):
        pl.semaphore_signal(
            barrier, inc=1, device_id={"py": flipped(py, o, n_py)}, device_id_type=MESH
        )

    def copy_y(f, o):
        to = flipped(py, o, n_py)
        return pltpu.make_async_remote_copy(
            src_ref=lines_out.at[f, to],
            dst_ref=lines.at[f, pl.ds(py * rows_y, rows_y)],
            send_sem=send_y.at[f, o],
            recv_sem=recv_y.at[f, o],
            device_id={"py": to},
            device_id_type=MESH,
        )

    def copy_z(f, o):
        to = flipped(pz, o, n_pz)
        return pltpu.make_async_remote_copy(
            src_ref=parts_out.at[f, pl.ds(to * rows_z, rows_z)],
            dst_ref=parts.at[f, pl.ds(pz * rows_z, rows_z)],
            send_sem=send_z.at[f, o],
            recv_sem=recv_z.at[f, o],
            device_id={"pz": to},
            device_id_type=MESH,
        )

    hx_copy.wait()
    for f in range(fields):
        load(f).wait()
        high, low = split(held[f])
        both = dot(jnp.concatenate([high, low], axis=0), hx[0])
        result = both[:rows_y] + both[rows_y:] + dot(high, hx[1])
        for d in range(n_py):
            lines_out[f, d] = result[:, d * share_x : (d + 1) * share_x]
        if f == 0:
            pl.semaphore_wait(barrier, n_py + n_pz - 2)
        for o in range(n_py - 1, 0, -1):
            copy_y(f, o).start()
        lines[f, pl.ds(py * rows_y, rows_y)] = lines_out[f, py]

    def iota(shape, dim):
        return lax.broadcasted_iota(jnp.int32, shape, dim)

    row, col = iota((depth_y, ny), 0), iota((depth_y, ny), 1)
    pick = (row // zl == col).astype(F32).astype(BF16)
    row, col = iota((ny, depth_y), 0), iota((ny, depth_y), 1)
    spread = (col // zl == row).astype(F32).astype(BF16)
    row, col = iota((depth_y, depth_y), 0), iota((depth_y, depth_y), 1)
    keep = row % zl == col % zl
    for t in range(2):
        wide = dot(dot(pick, hy_ref[t]).astype(BF16), spread)
        my[t] = jnp.where(keep, wide, 0.0).astype(BF16)
    row, col = iota((rows_out, nz), 0), iota((rows_out, nz), 1)
    pick = (row % nz == col).astype(F32).astype(BF16)
    row, col = iota((nz, depth_z), 0), iota((nz, depth_z), 1)
    spread = ((col // rows_z) * zl + col % zl == row).astype(F32).astype(BF16)
    row, col = iota((rows_out, depth_z), 0), iota((rows_out, depth_z), 1)
    keep = row // nz == (col // zl) % share_y
    for t in range(2):
        wide = dot(dot(pick, hz_ref[t]).astype(BF16), spread)
        mz[t] = jnp.where(keep, wide, 0.0).astype(BF16)

    def rows_transform(table, values):
        high, low = split(values)
        both = dot(table[0], jnp.concatenate([high, low], axis=1))
        return both[:, :share_x] + both[:, share_x:] + dot(table[1], high)

    for f in range(fields):
        for o in range(n_py - 1, 0, -1):
            copy_y(f, o).wait_recv()
        parts_out[f] = rows_transform(my, lines[f])
        for o in range(n_pz - 1, 0, -1):
            copy_z(f, o).start()
        parts[f, pl.ds(pz * rows_z, rows_z)] = parts_out[f, pl.ds(pz * rows_z, rows_z)]

    diagonal = iota((nz, nz), 0) == iota((nz, nz), 1)
    sz_column = jnp.sum(jnp.where(diagonal, sz_ref[...], 0.0), axis=1, keepdims=True)
    sx_row = sx_ref[:, pl.ds(pl.multiple_of(py * share_x, share_x), share_x)]

    for f in range(fields):
        for o in range(n_pz - 1, 0, -1):
            copy_z(f, o).wait_recv()
        modes[f] = rows_transform(mz, parts[f])
    for k in range(share_y):
        span = pl.ds(k * nz, nz)
        weight = 1.0 / (1.0 + ((sx_row + sy_ref[pz * share_y + k]) + sz_column))
        old = [modes[f, span] for f in range(fields)]
        for a in range(fields):
            mixed = coupling_ref[a, 0] * old[0]
            for b in range(1, fields):
                mixed = mixed + coupling_ref[a, b] * old[b]
            out_ref[a, span] = weight * old[a] + (1.0 - weight) * mixed
    for f in range(fields):
        for o in range(1, n_py):
            copy_y(f, o).wait_send()
        for o in range(1, n_pz):
            copy_z(f, o).wait_send()


def shards(n_py, n_pz, species, coupling, symbol_x, symbol_y, symbol_z):
    fields, nx, yl, zl = species.shape
    ny, nz = yl * n_py, zl * n_pz
    share_x, share_y = nx // n_py, ny // n_pz
    block = fields * nx * yl * zl
    tables = 2 * (nx * nx + (ny * zl) ** 2 + (share_y * nz) ** 2)
    need = 7 * 4 * block + 2 * tables + 16 * max(ny * zl, share_y * nz) ** 2
    if share_x % LANES or zl % SUBLANES or nx % n_py or ny % n_pz or need > VMEM_BUDGET:
        return plain_shards(species, coupling, symbol_x, symbol_y, symbol_z)
    dims = (fields, ny, nz, n_py, n_pz, yl, zl, share_x, share_y)
    rows_y, depth_y, depth_z = yl * zl, ny * zl, share_y * nz
    vmem = pl.BlockSpec(memory_space=pltpu.VMEM)
    smem = pl.BlockSpec(memory_space=pltpu.SMEM)
    anywhere = pl.BlockSpec(memory_space=pl.ANY)
    values = jnp.transpose(species, (0, 2, 3, 1)).reshape(fields, rows_y, nx)
    out = pl.pallas_call(
        functools.partial(kernel, dims),
        out_shape=jax.ShapeDtypeStruct((fields, depth_z, share_x), F32),
        in_specs=[anywhere, anywhere, vmem, vmem, smem, vmem, smem, vmem],
        out_specs=vmem,
        scratch_shapes=[
            pltpu.VMEM((fields, rows_y, nx), F32),
            pltpu.VMEM((2, nx, nx), BF16),
            pltpu.VMEM((fields, n_py, rows_y, share_x), F32),
            pltpu.VMEM((fields, depth_y, share_x), F32),
            pltpu.VMEM((fields, depth_y, share_x), F32),
            pltpu.VMEM((fields, depth_z, share_x), F32),
            pltpu.VMEM((fields, depth_z, share_x), F32),
            pltpu.VMEM((2, depth_y, depth_y), BF16),
            pltpu.VMEM((2, depth_z, depth_z), BF16),
            pltpu.SemaphoreType.DMA((fields,)),
            pltpu.SemaphoreType.DMA,
            pltpu.SemaphoreType.DMA((fields, n_py)),
            pltpu.SemaphoreType.DMA((fields, n_py)),
            pltpu.SemaphoreType.DMA((fields, n_pz)),
            pltpu.SemaphoreType.DMA((fields, n_pz)),
        ],
        compiler_params=pltpu.CompilerParams(
            collective_id=0, has_side_effects=True, vmem_limit_bytes=VMEM_BUDGET
        ),
    )(
        values,
        jnp.asarray(split_table(nx)),
        jnp.asarray(split_table(ny)),
        jnp.asarray(split_table(nz)),
        coupling,
        symbol_x.reshape(1, nx),
        symbol_y,
        symbol_z.reshape(1, nz),
    )
    return jnp.transpose(out.reshape(fields, share_y, nz, share_x), (0, 3, 1, 2))


def solution(mesh):
    return jax.shard_map(
        functools.partial(shards, mesh.shape["py"], mesh.shape["pz"]),
        mesh=mesh,
        in_specs=(P(None, None, "py", "pz"), P(), P(), P(), P()),
        out_specs=P(None, "py", "pz", None),
        check_vma=False,
    )
```

time: 95.4 us -> 41.8 us (0.44)
  waiting for transfers between devices: 39.1 us -> 0 us
  Pallas kernels: 0 us -> 36.6 us
  local copies, waits for them, and re-layouts: 29.3 us -> 4.88 us
  matrix products: 11.2 us -> 0 us
  starting transfers between devices: 10.1 us -> 0 us
  other arithmetic: 5.07 us -> 0 us
    all_to_all x2 -> x0, waiting for transfers between devices: 39.1 us -> none  [the longest x1 25.5 us: shards(): lax.all_to_all(pencil_values, 'pz', split_axis=2, concat_axis=3, tiled=True)]
    pallas_call x0 -> x1, Pallas kernels: none -> 36.6 us  [shards(): pl.pallas_call(functools.partial(kernel, dims), out_shape=jax.ShapeDtypeS...]
    dot_general x4 -> x0, matrix products: 11.2 us -> none  [the longest x3 8.73 us: transform_dim(): jnp.tensordot(values, mode_table(values.shape[dim]), axes=([dim], [0]), p...]
    all_to_all x2 -> x0, starting transfers between devices: 10.1 us -> none  [the longest x1 5.19 us: shards(): lax.all_to_all(part_values, 'py', split_axis=1, concat_axis=2, tiled=True)]
    transpose x2 -> x0, local copies, waits for them, and re-layouts: 9.07 us -> none  [transform_dim(): return jnp.moveaxis(moved, -1, dim)]
    unnamed x10 -> x15, local copies, waits for them, and re-layouts: 13.8 us -> 4.88 us
    all_to_all x2 -> x0, local copies, waits for them, and re-layouts: 5.68 us -> none  [shards(): lax.all_to_all(part_values, 'py', split_axis=1, concat_axis=2, tiled=True)]
    all_to_all x1 -> x0, other arithmetic: 3.68 us -> none  [shards(): lax.all_to_all(part_values, 'py', split_axis=1, concat_axis=2, tiled=True)]
  transfers between devices with their start and end apart: 2 -> 0, of which waited for: 2 -> 0; matrix products, arithmetic and copies ran while one was open for 1% -> 0% of each run, Pallas kernels for 0% -> 0%
where the time goes in v1:
time: 41.8 us; the launch traced here: 41.5 us
  Pallas kernels  36.6 us (88%)
  local copies, waits for them, and re-layouts  4.88 us (12%)
    pallas_call x1, Pallas kernels, shards(): pl.pallas_call(functools.partial(kernel, dims), out_shape=jax.ShapeDtypeS...  36.6 us
    unnamed x15, local copies, waits for them, and re-layouts  4.88 us

profile of v1, /device:TPU:0, one launch (start us, length us, event | category | flops | bytes accessed | tf_op | source)
XLA Modules:
  0.0 41.5 jit_solution(1746086719752864279)
XLA Ops:
  0.0 0.0 copy-start.4
  0.0 0.0 copy-start.3
  0.0 0.0 copy-start.5
  0.0 0.0 copy-start.6
  0.0 0.7 %copy-done.4 = f32[512]{0:T(512)S(1)} copy-done((f32[512]{0:T(512)S(1)}, f32[512]{0:T(512)}, u32[]{:S(2)}) %copy-start.4) | copy-done | bytes 2072
  0.7 0.0 copy-done.3
  0.7 0.0 copy-done.5
  0.7 0.0 copy-done.6
  0.7 0.0 copy-start
  0.7 1.2 %copy-done = f32[4,512,16,8]{1,3,2,0:T(8,128)S(1)} copy-done((f32[4,512,16,8]{1,3,2,0:T(8,128)S(1)}, f32[4,512,16,8]{1,3,2,0:T(8,128)}, u32[]{:S(2)}) %copy-start) | copy-done | bytes 1048600
  1.9 0.0 copy-start.1
  1.9 1.2 %copy-done.1 = bf16[2,512,512]{2,1,0:T(8,128)(2,1)S(1)} copy-done((bf16[2,512,512]{2,1,0:T(8,128)(2,1)S(1)}, bf16[2,512,512]{2,1,0:T(8,128)(2,1)}, u32[]{:S(2)}) %copy-start.1) | copy-done | bytes 1048600
  3.2 0.0 copy-start.2
  3.2 0.8 %copy-done.2 = bf16[2,64,64]{2,1,0:T(8,128)(2,1)S(1)} copy-done((bf16[2,64,64]{2,1,0:T(8,128)(2,1)S(1)}, bf16[2,64,64]{2,1,0:T(8,128)(2,1)}, u32[]{:S(2)}) %copy-start.2) | copy-done | bytes 16408
  3.9 36.6 %shard_map.82 = f32[4,512,128]{2,1,0:T(8,128)S(1)} custom-call(f32[4,128,512]{2,1,0:T(8,128)S(1)} %bitcast.9, bf16[2,512,512]{2,1,0:T(8,128)(2,1)S(1)} %copy-done.1, bf16[2,64,64]{2,1,0:T(8,128)(2,1)S(1)} %copy-done.2, bf16[2,64,64]{2,1,0:T(8,128)(2,1)S(1)} %copy-done.2, f32[4,4]{1,0:T(4,128)S(1)} %copy-done.3, f32[1,512]{1,0:T(1,128)S(1)} %bitcast.10, ...), custom_call_target="tpu_custom_call" | custom-call | tf_op jit(solution)/shard_map/pallas_call | solution.py:229
  40.5 1.0 %copy.10 = f32[4,128,8,64]{1,3,2,0:T(8,128)} copy(f32[4,128,8,64]{1,3,2,0:T(8,128)S(1)} %bitcast.8) | data formatting | bytes 2097152
Async XLA Ops:
  0.0 0.7 %copy-start.4 = (f32[512]{0:T(512)S(1)}, f32[512]{0:T(512)}, u32[]{:S(2)}) copy-start(f32[512]{0:T(512)} %param.10) | copy-start | bytes 6148
  0.0 0.7 %copy-start.3 = (f32[4,4]{1,0:T(4,128)S(1)}, f32[4,4]{1,0:T(4,128)}, u32[]{:S(2)}) copy-start(f32[4,4]{1,0:T(4,128)} %coupling_ref.1) | copy-start | bytes 196
  0.0 0.7 %copy-start.5 = (f32[64]{0:T(128)S(1)}, f32[64]{0:T(128)}, u32[]{:S(2)}) copy-start(f32[64]{0:T(128)} %sy_ref.1) | copy-start | bytes 772
  0.0 0.7 %copy-start.6 = (f32[64]{0:T(128)S(1)}, f32[64]{0:T(128)}, u32[]{:S(2)}) copy-start(f32[64]{0:T(128)} %param.12) | copy-start | bytes 772
  0.7 1.2 %copy-start = (f32[4,512,16,8]{1,3,2,0:T(8,128)S(1)}, f32[4,512,16,8]{1,3,2,0:T(8,128)}, u32[]{:S(2)}) copy-start(f32[4,512,16,8]{1,3,2,0:T(8,128)} %param.8) | copy-start | bytes 3145732
  1.9 1.2 %copy-start.1 = (bf16[2,512,512]{2,1,0:T(8,128)(2,1)S(1)}, bf16[2,512,512]{2,1,0:T(8,128)(2,1)}, u32[]{:S(2)}) copy-start(bf16[2,512,512]{2,1,0:T(8,128)(2,1)} %constant.4.clone.hx_hbm) | copy-start | bytes 3145732
  3.2 0.8 %copy-start.2 = (bf16[2,64,64]{2,1,0:T(8,128)(2,1)S(1)}, bf16[2,64,64]{2,1,0:T(8,128)(2,1)}, u32[]{:S(2)}) copy-start(bf16[2,64,64]{2,1,0:T(8,128)(2,1)} %constant.5.clone.hy_ref.hz_ref) | copy-start | bytes 49156

commit v2 on v1

--- a/solution.py
+++ b/solution.py
@@ -86,9 +86,9 @@
 
 
 def kernel(
-    dims, field_ref, hx_hbm, hy_ref, hz_ref, coupling_ref, sx_ref, sy_ref, sz_ref, out_ref,
-    held, hx, lines_out, lines, parts_out, parts, modes, my, mz,
-    load_sem, hx_sem, send_y, recv_y, send_z, recv_z,
+    dims, field_ref, hx_hbm, hy_hbm, hz_hbm, coupling_hbm, sx_hbm, sy_hbm, sz_hbm, out_ref,
+    held, hx, hy, hz, coupling, sx, sy, sz, lines_out, lines, parts_out, parts, modes, weights,
+    my, mz, load_sem, side_sem, send_y, recv_y, send_z, recv_z,
 ):
     fields, ny, nz, n_py, n_pz, yl, zl, share_x, share_y = dims
     py, pz = lax.axis_index("py"), lax.axis_index("pz")
@@ -101,11 +101,20 @@
     def load(f):
         return pltpu.make_async_copy(field_ref.at[f], held.at[f], load_sem.at[f])
 
-    hx_copy = pltpu.make_async_copy(hx_hbm, hx, hx_sem)
+    pairs = (
+        (hx_hbm.at[0], hx.at[0]), (hx_hbm.at[1], hx.at[1]), (hy_hbm, hy), (hz_hbm, hz),
+        (coupling_hbm, coupling), (sx_hbm, sx), (sy_hbm, sy), (sz_hbm, sz),
+    )
+    sides = [
+        pltpu.make_async_copy(a, b, side_sem.at[i]) for i, (a, b) in enumerate(pairs)
+    ]
     load(0).start()
-    hx_copy.start()
+    sides[0].start()
+    sides[1].start()
     for f in range(1, fields):
         load(f).start()
+    for side in sides[2:]:
+        side.start()
     barrier = pltpu.get_barrier_semaphore()
     for o in range(1, n_pz):
         pl.semaphore_signal(
@@ -138,10 +147,12 @@
             device_id_type=MESH,
         )
 
-    hx_copy.wait()
     for f in range(fields):
         load(f).wait()
         high, low = split(held[f])
+        if f == 0:
+            sides[0].wait()
+            sides[1].wait()
         both = dot(jnp.concatenate([high, low], axis=0), hx[0])
         result = both[:rows_y] + both[rows_y:] + dot(high, hx[1])
         for d in range(n_py):
@@ -152,6 +163,9 @@
             copy_y(f, o).start()
         lines[f, pl.ds(py * rows_y, rows_y)] = lines_out[f, py]
 
+    for side in sides[2:]:
+        side.wait()
+
     def iota(shape, dim):
         return lax.broadcasted_iota(jnp.int32, shape, dim)
 
@@ -162,8 +176,27 @@
     row, col = iota((depth_y, depth_y), 0), iota((depth_y, depth_y), 1)
     keep = row % zl == col % zl
     for t in range(2):
-        wide = dot(dot(pick, hy_ref[t]).astype(BF16), spread)
+        wide = dot(dot(pick, hy[t]).astype(BF16), spread)
         my[t] = jnp.where(keep, wide, 0.0).astype(BF16)
+    def rows_transform(high_table, low_table, high, low):
+        both = dot(high_table, jnp.concatenate([high, low], axis=1))
+        return both[:, :share_x] + both[:, share_x:] + dot(low_table, high)
+
+    halves = 2 if n_pz % 2 == 0 and n_pz & (n_pz - 1) == 0 else 1
+    half_rows = depth_y // halves
+    for f in range(fields):
+        for o in range(n_py - 1, 0, -1):
+            copy_y(f, o).wait_recv()
+        high, low = split(lines[f])
+        for h in range(halves):
+            part = lax.rem(pz // (n_pz // halves) + h + 1, halves)
+            span = pl.ds(pl.multiple_of(part * half_rows, half_rows), half_rows)
+            parts_out[f, span] = rows_transform(my[0, span], my[1, span], high, low)
+            top = n_pz - h * (n_pz // halves)
+            for o in range(top - 1, max(top - n_pz // halves, 1) - 1, -1):
+                copy_z(f, o).start()
+        parts[f, pl.ds(pz * rows_z, rows_z)] = parts_out[f, pl.ds(pz * rows_z, rows_z)]
+
     row, col = iota((rows_out, nz), 0), iota((rows_out, nz), 1)
     pick = (row % nz == col).astype(F32).astype(BF16)
     row, col = iota((nz, depth_z), 0), iota((nz, depth_z), 1)
@@ -171,39 +204,41 @@
     row, col = iota((rows_out, depth_z), 0), iota((rows_out, depth_z), 1)
     keep = row // nz == (col // zl) % share_y
     for t in range(2):
-        wide = dot(dot(pick, hz_ref[t]).astype(BF16), spread)
+        wide = dot(dot(pick, hz[t]).astype(BF16), spread)
         mz[t] = jnp.where(keep, wide, 0.0).astype(BF16)
 
-    def rows_transform(table, values):
-        high, low = split(values)
-        both = dot(table[0], jnp.concatenate([high, low], axis=1))
-        return both[:, :share_x] + both[:, share_x:] + dot(table[1], high)
-
-    for f in range(fields):
-        for o in range(n_py - 1, 0, -1):
-            copy_y(f, o).wait_recv()
-        parts_out[f] = rows_transform(my, lines[f])
-        for o in range(n_pz - 1, 0, -1):
-            copy_z(f, o).start()
-        parts[f, pl.ds(pz * rows_z, rows_z)] = parts_out[f, pl.ds(pz * rows_z, rows_z)]
-
     diagonal = iota((nz, nz), 0) == iota((nz, nz), 1)
-    sz_column = jnp.sum(jnp.where(diagonal, sz_ref[...], 0.0), axis=1, keepdims=True)
-    sx_row = sx_ref[:, pl.ds(pl.multiple_of(py * share_x, share_x), share_x)]
-
+    sz_column = jnp.sum(jnp.where(diagonal, sz[...], 0.0), axis=1, keepdims=True)
+    sx_row = sx[:, pl.ds(pl.multiple_of(py * share_x, share_x), share_x)]
+    for k in range(share_y):
+        symbol = (sx_row + sy[pz * share_y + k]) + sz_column
+        weights[pl.ds(k * nz, nz)] = 1.0 / (1.0 + symbol)
+
+    last = fields - 1
     for f in range(fields):
         for o in range(n_pz - 1, 0, -1):
             copy_z(f, o).wait_recv()
-        modes[f] = rows_transform(mz, parts[f])
-    for k in range(share_y):
-        span = pl.ds(k * nz, nz)
-        weight = 1.0 / (1.0 + ((sx_row + sy_ref[pz * share_y + k]) + sz_column))
-        old = [modes[f, span] for f in range(fields)]
-        for a in range(fields):
-            mixed = coupling_ref[a, 0] * old[0]
-            for b in range(1, fields):
-                mixed = mixed + coupling_ref[a, b] * old[b]
-            out_ref[a, span] = weight * old[a] + (1.0 - weight) * mixed
+        high, low = split(parts[f])
+        if f < last:
+            modes[f] = rows_transform(mz[0], mz[1], high, low)
+        if f == last - 1:
+            for k in range(share_y):
+                span = pl.ds(k * nz, nz)
+                weight = weights[span]
+                old = [modes[b, span] for b in range(last)]
+                for a in range(fields):
+                    mixed = coupling[a, 0] * old[0]
+                    for b in range(1, last):
+                        mixed = mixed + coupling[a, b] * old[b]
+                    mixed = (1.0 - weight) * mixed
+                    out_ref[a, span] = mixed + weight * old[a] if a < last else mixed
+        if f == last:
+            result = rows_transform(mz[0], mz[1], high, low)
+            weight = weights[...]
+            rest = (1.0 - weight) * result
+            for a in range(fields):
+                new = out_ref[a] + coupling[a, last] * rest
+                out_ref[a] = new + weight * result if a == last else new
     for f in range(fields):
         for o in range(1, n_py):
             copy_y(f, o).wait_send()
@@ -218,31 +253,37 @@
     block = fields * nx * yl * zl
     tables = 2 * (nx * nx + (ny * zl) ** 2 + (share_y * nz) ** 2)
     need = 7 * 4 * block + 2 * tables + 16 * max(ny * zl, share_y * nz) ** 2
-    if share_x % LANES or zl % SUBLANES or nx % n_py or ny % n_pz or need > VMEM_BUDGET:
+    if share_x % LANES or zl % SUBLANES or nx % n_py or ny % n_pz or need > VMEM_BUDGET or fields < 2:
         return plain_shards(species, coupling, symbol_x, symbol_y, symbol_z)
     dims = (fields, ny, nz, n_py, n_pz, yl, zl, share_x, share_y)
     rows_y, depth_y, depth_z = yl * zl, ny * zl, share_y * nz
     vmem = pl.BlockSpec(memory_space=pltpu.VMEM)
-    smem = pl.BlockSpec(memory_space=pltpu.SMEM)
-    anywhere = pl.BlockSpec(memory_space=pl.ANY)
+    hbm = pl.BlockSpec(memory_space=pltpu.HBM)
     values = jnp.transpose(species, (0, 2, 3, 1)).reshape(fields, rows_y, nx)
     out = pl.pallas_call(
         functools.partial(kernel, dims),
         out_shape=jax.ShapeDtypeStruct((fields, depth_z, share_x), F32),
-        in_specs=[anywhere, anywhere, vmem, vmem, smem, vmem, smem, vmem],
+        in_specs=[hbm] * 8,
         out_specs=vmem,
         scratch_shapes=[
             pltpu.VMEM((fields, rows_y, nx), F32),
             pltpu.VMEM((2, nx, nx), BF16),
+            pltpu.VMEM((2, ny, ny), BF16),
+            pltpu.VMEM((2, nz, nz), BF16),
+            pltpu.SMEM((fields, fields), F32),
+            pltpu.VMEM((1, nx), F32),
+            pltpu.SMEM((ny,), F32),
+            pltpu.VMEM((1, nz), F32),
             pltpu.VMEM((fields, n_py, rows_y, share_x), F32),
             pltpu.VMEM((fields, depth_y, share_x), F32),
             pltpu.VMEM((fields, depth_y, share_x), F32),
             pltpu.VMEM((fields, depth_z, share_x), F32),
-            pltpu.VMEM((fields, depth_z, share_x), F32),
+            pltpu.VMEM((fields - 1, depth_z, share_x), F32),
+            pltpu.VMEM((depth_z, share_x), F32),
             pltpu.VMEM((2, depth_y, depth_y), BF16),
             pltpu.VMEM((2, depth_z, depth_z), BF16),
             pltpu.SemaphoreType.DMA((fields,)),
-            pltpu.SemaphoreType.DMA,
+            pltpu.SemaphoreType.DMA((8,)),
             pltpu.SemaphoreType.DMA((fields, n_py)),
             pltpu.SemaphoreType.DMA((fields, n_py)),
             pltpu.SemaphoreType.DMA((fields, n_pz)),

time: 41.8 us -> 41 us (0.981)
  Pallas kernels: 36.6 us -> 35.8 us
    pallas_call x1, Pallas kernels: 36.6 us -> 35.8 us  [shards(): pl.pallas_call(functools.partial(kernel, dims), out_shape=jax.ShapeDtypeS...]
where the time goes in v2:
time: 41 us; the launch traced here: 40.7 us
  Pallas kernels  35.8 us (87%)
  local copies, waits for them, and re-layouts  4.88 us (12%)
    pallas_call x1, Pallas kernels, shards(): pl.pallas_call(functools.partial(kernel, dims), out_shape=jax.ShapeDtypeS...  35.8 us
    unnamed x15, local copies, waits for them, and re-layouts  4.88 us

profile of v2, /device:TPU:0, one launch (start us, length us, event | category | flops | bytes accessed | tf_op | source)
XLA Modules:
  0.0 40.7 jit_solution(2339829089180580606)
XLA Ops:
  0.0 0.0 copy-start.4
  0.0 0.0 copy-start.3
  0.0 0.0 copy-start.5
  0.0 0.0 copy-start.6
  0.0 0.7 %copy-done.4 = f32[512]{0:T(512)S(1)} copy-done((f32[512]{0:T(512)S(1)}, f32[512]{0:T(512)}, u32[]{:S(2)}) %copy-start.4) | copy-done | bytes 2072
  0.7 0.0 copy-done.3
  0.7 0.0 copy-done.5
  0.7 0.0 copy-done.6
  0.7 0.0 copy-start
  0.7 1.2 %copy-done = f32[4,512,16,8]{1,3,2,0:T(8,128)S(1)} copy-done((f32[4,512,16,8]{1,3,2,0:T(8,128)S(1)}, f32[4,512,16,8]{1,3,2,0:T(8,128)}, u32[]{:S(2)}) %copy-start) | copy-done | bytes 1048600
  1.9 0.0 copy-start.1
  1.9 1.2 %copy-done.1 = bf16[2,512,512]{2,1,0:T(8,128)(2,1)S(1)} copy-done((bf16[2,512,512]{2,1,0:T(8,128)(2,1)S(1)}, bf16[2,512,512]{2,1,0:T(8,128)(2,1)}, u32[]{:S(2)}) %copy-start.1) | copy-done | bytes 1048600
  3.2 0.0 copy-start.2
  3.2 0.8 %copy-done.2 = bf16[2,64,64]{2,1,0:T(8,128)(2,1)S(1)} copy-done((bf16[2,64,64]{2,1,0:T(8,128)(2,1)S(1)}, bf16[2,64,64]{2,1,0:T(8,128)(2,1)}, u32[]{:S(2)}) %copy-start.2) | copy-done | bytes 16408
  3.9 35.8 %shard_map.82 = f32[4,512,128]{2,1,0:T(8,128)S(1)} custom-call(f32[4,128,512]{2,1,0:T(8,128)S(1)} %bitcast.9, bf16[2,512,512]{2,1,0:T(8,128)(2,1)S(1)} %copy-done.1, bf16[2,64,64]{2,1,0:T(8,128)(2,1)S(1)} %copy-done.2, bf16[2,64,64]{2,1,0:T(8,128)(2,1)S(1)} %copy-done.2, f32[4,4]{1,0:T(4,128)S(1)} %copy-done.3, f32[1,512]{1,0:T(1,128)S(1)} %bitcast.10, ...), custom_call_target="tpu_custom_call" | custom-call | tf_op jit(solution)/shard_map/pallas_call | solution.py:263
  39.7 1.0 %copy.10 = f32[4,128,8,64]{1,3,2,0:T(8,128)} copy(f32[4,128,8,64]{1,3,2,0:T(8,128)S(1)} %bitcast.8) | data formatting | bytes 2097152
Async XLA Ops:
  0.0 0.7 %copy-start.4 = (f32[512]{0:T(512)S(1)}, f32[512]{0:T(512)}, u32[]{:S(2)}) copy-start(f32[512]{0:T(512)} %param.10) | copy-start | bytes 6148
  0.0 0.7 %copy-start.3 = (f32[4,4]{1,0:T(4,128)S(1)}, f32[4,4]{1,0:T(4,128)}, u32[]{:S(2)}) copy-start(f32[4,4]{1,0:T(4,128)} %coupling_hbm.1) | copy-start | bytes 196
  0.0 0.7 %copy-start.5 = (f32[64]{0:T(128)S(1)}, f32[64]{0:T(128)}, u32[]{:S(2)}) copy-start(f32[64]{0:T(128)} %sy_hbm.1) | copy-start | bytes 772
  0.0 0.7 %copy-start.6 = (f32[64]{0:T(128)S(1)}, f32[64]{0:T(128)}, u32[]{:S(2)}) copy-start(f32[64]{0:T(128)} %param.12) | copy-start | bytes 772
  0.7 1.2 %copy-start = (f32[4,512,16,8]{1,3,2,0:T(8,128)S(1)}, f32[4,512,16,8]{1,3,2,0:T(8,128)}, u32[]{:S(2)}) copy-start(f32[4,512,16,8]{1,3,2,0:T(8,128)} %param.8) | copy-start | bytes 3145732
  1.9 1.2 %copy-start.1 = (bf16[2,512,512]{2,1,0:T(8,128)(2,1)S(1)}, bf16[2,512,512]{2,1,0:T(8,128)(2,1)}, u32[]{:S(2)}) copy-start(bf16[2,512,512]{2,1,0:T(8,128)(2,1)} %constant.4.clone.hx_hbm) | copy-start | bytes 3145732
  3.2 0.8 %copy-start.2 = (bf16[2,64,64]{2,1,0:T(8,128)(2,1)S(1)}, bf16[2,64,64]{2,1,0:T(8,128)(2,1)}, u32[]{:S(2)}) copy-start(bf16[2,64,64]{2,1,0:T(8,128)(2,1)} %constant.5.clone.hy_hbm.hz_hbm) | copy-start | bytes 49156

commit v3 on v2

--- a/solution.py
+++ b/solution.py
@@ -290,7 +290,7 @@
             pltpu.SemaphoreType.DMA((fields, n_pz)),
         ],
         compiler_params=pltpu.CompilerParams(
-            collective_id=0, has_side_effects=True, vmem_limit_bytes=VMEM_BUDGET
+            collective_id=0, has_side_effects=True, vmem_limit_bytes=67043328
         ),
     )(
         values,

time: 41 us -> 39 us (0.951)
  local copies, waits for them, and re-layouts: 4.88 us -> 2.31 us
  Pallas kernels: 35.8 us -> 36.5 us
    unnamed x15 -> x1, local copies, waits for them, and re-layouts: 4.88 us -> 2.31 us
    pallas_call x1, Pallas kernels: 35.8 us -> 36.5 us  [shards(): pl.pallas_call(functools.partial(kernel, dims), out_shape=jax.ShapeDtypeS...]
where the time goes in v3:
time: 39 us; the launch traced here: 38.8 us
  Pallas kernels  36.5 us (94%)
  local copies, waits for them, and re-layouts  2.31 us (6%)
    pallas_call x1, Pallas kernels, shards(): pl.pallas_call(functools.partial(kernel, dims), out_shape=jax.ShapeDtypeS...  36.5 us
    unnamed x1, local copies, waits for them, and re-layouts  2.31 us

profile of v3, /device:TPU:0, one launch (start us, length us, event | category | flops | bytes accessed | tf_op | source)
XLA Modules:
  0.0 38.8 jit_solution(13611508345067542834)
XLA Ops:
  0.0 36.5 %shard_map.82 = f32[4,512,128]{2,1,0:T(8,128)} custom-call(f32[4,128,512]{2,1,0:T(8,128)} %bitcast.9, bf16[2,512,512]{2,1,0:T(8,128)(2,1)} %constant.4.clone.hx_hbm, bf16[2,64,64]{2,1,0:T(8,128)(2,1)} %constant.5.clone.hy_hbm.hz_hbm, bf16[2,64,64]{2,1,0:T(8,128)(2,1)} %constant.5.clone.hy_hbm.hz_hbm, f32[4,4]{1,0:T(4,128)} %coupling_hbm.1, ...), custom_call_target="tpu_custom_call" | custom-call | tf_op jit(solution)/shard_map/pallas_call | solution.py:263
  36.5 2.3 %copy.10 = f32[4,128,8,64]{1,3,2,0:T(8,128)} copy(f32[4,128,8,64]{1,3,2,0:T(8,128)} %bitcast.8) | data formatting | bytes 2097152

commit v4 on v3

--- a/solution.py
+++ b/solution.py
@@ -12,6 +12,7 @@
 F32 = jnp.float32
 BF16 = jnp.bfloat16
 LANES, SUBLANES = 128, 8
+CUTS = 2
 VMEM_BUDGET = 48 << 20
 
 
@@ -92,14 +93,22 @@
 ):
     fields, ny, nz, n_py, n_pz, yl, zl, share_x, share_y = dims
     py, pz = lax.axis_index("py"), lax.axis_index("pz")
-    rows_y = yl * zl
-    rows_z = share_y * zl
-    depth_y = ny * zl
+    zc = zl // CUTS
+    rows_y = yl * zc
+    rows_z = share_y * zc
+    depth_y = ny * zc
     rows_out = share_y * nz
-    depth_z = n_pz * rows_z
+    depth_z = n_pz * rows_z * CUTS
+
+    columns = field_ref.shape[2] // LANES
 
     def load(f):
-        return pltpu.make_async_copy(field_ref.at[f], held.at[f], load_sem.at[f])
+        return [
+            pltpu.make_async_copy(
+                field_ref.at[f, :, pl.ds(j * LANES, LANES)], held.at[f, j], load_sem.at[f, j]
+            )
+            for j in range(columns)
+        ]
 
     pairs = (
         (hx_hbm.at[0], hx.at[0]), (hx_hbm.at[1], hx.at[1]), (hy_hbm, hy), (hz_hbm, hz),
@@ -108,11 +117,13 @@
     sides = [
         pltpu.make_async_copy(a, b, side_sem.at[i]) for i, (a, b) in enumerate(pairs)
     ]
-    load(0).start()
+    for part in load(0):
+        part.start()
     sides[0].start()
     sides[1].start()
     for f in range(1, fields):
-        load(f).start()
+        for part in load(f):
+            part.start()
     for side in sides[2:]:
         side.start()
     barrier = pltpu.get_barrier_semaphore()
@@ -125,43 +136,56 @@
             barrier, inc=1, device_id={"py": flipped(py, o, n_py)}, device_id_type=MESH
         )
 
-    def copy_y(f, o):
+    def copy_y(f, c, o):
         to = flipped(py, o, n_py)
         return pltpu.make_async_remote_copy(
-            src_ref=lines_out.at[f, to],
-            dst_ref=lines.at[f, pl.ds(py * rows_y, rows_y)],
-            send_sem=send_y.at[f, o],
-            recv_sem=recv_y.at[f, o],
+            src_ref=lines_out.at[f, c, to],
+            dst_ref=lines.at[f, c, pl.ds(py * rows_y, rows_y)],
+            send_sem=send_y.at[f * CUTS + c, o],
+            recv_sem=recv_y.at[f * CUTS + c, o],
             device_id={"py": to},
             device_id_type=MESH,
         )
 
-    def copy_z(f, o):
+    def copy_z(f, c, o):
         to = flipped(pz, o, n_pz)
         return pltpu.make_async_remote_copy(
-            src_ref=parts_out.at[f, pl.ds(to * rows_z, rows_z)],
-            dst_ref=parts.at[f, pl.ds(pz * rows_z, rows_z)],
-            send_sem=send_z.at[f, o],
-            recv_sem=recv_z.at[f, o],
+            src_ref=parts_out.at[f, c, pl.ds(to * rows_z, rows_z)],
+            dst_ref=parts.at[f, pl.ds((pz * CUTS + c) * rows_z, rows_z)],
+            send_sem=send_z.at[f * CUTS + c, o],
+            recv_sem=recv_z.at[f * CUTS + c, o],
             device_id={"pz": to},
             device_id_type=MESH,
         )
 
     for f in range(fields):
-        load(f).wait()
-        high, low = split(held[f])
-        if f == 0:
-            sides[0].wait()
-            sides[1].wait()
-        both = dot(jnp.concatenate([high, low], axis=0), hx[0])
-        result = both[:rows_y] + both[rows_y:] + dot(high, hx[1])
-        for d in range(n_py):
-            lines_out[f, d] = result[:, d * share_x : (d + 1) * share_x]
-        if f == 0:
-            pl.semaphore_wait(barrier, n_py + n_pz - 2)
-        for o in range(n_py - 1, 0, -1):
-            copy_y(f, o).start()
-        lines[f, pl.ds(py * rows_y, rows_y)] = lines_out[f, py]
+        for part in load(f):
+            part.wait()
+        batches = [[c] for c in range(CUTS)] if f == 0 else [list(range(CUTS))]
+        for batch in batches:
+            span = range(batch[0] * zc, (batch[-1] + 1) * zc)
+            blocks = [
+                jnp.concatenate([held[f, j, pl.ds(z, yl, stride=zl)] for z in span], axis=0)
+                for j in range(columns)
+            ]
+            high, low = split(jnp.concatenate(blocks, axis=1))
+            count = len(batch) * rows_y
+            if f == 0 and batch[0] == 0:
+                sides[0].wait()
+                sides[1].wait()
+            both = dot(jnp.concatenate([high, low], axis=0), hx[0])
+            result = both[:count] + both[count:] + dot(high, hx[1])
+            for i, c in enumerate(batch):
+                for d in range(n_py):
+                    lines_out[f, c, d] = result[
+                        i * rows_y : (i + 1) * rows_y, d * share_x : (d + 1) * share_x
+                    ]
+            if f == 0 and batch[0] == 0:
+                pl.semaphore_wait(barrier, n_py + n_pz - 2)
+            for c in batch:
+                for o in range(n_py - 1, 0, -1):
+                    copy_y(f, c, o).start()
+                lines[f, c, pl.ds(py * rows_y, rows_y)] = lines_out[f, c, py]
 
     for side in sides[2:]:
         side.wait()
@@ -170,11 +194,11 @@
         return lax.broadcasted_iota(jnp.int32, shape, dim)
 
     row, col = iota((depth_y, ny), 0), iota((depth_y, ny), 1)
-    pick = (row // zl == col).astype(F32).astype(BF16)
+    pick = (row // zc == col).astype(F32).astype(BF16)
     row, col = iota((ny, depth_y), 0), iota((ny, depth_y), 1)
-    spread = (col // zl == row).astype(F32).astype(BF16)
+    spread = ((col // rows_y) * yl + col % yl == row).astype(F32).astype(BF16)
     row, col = iota((depth_y, depth_y), 0), iota((depth_y, depth_y), 1)
-    keep = row % zl == col % zl
+    keep = row % zc == (col // yl) % zc
     for t in range(2):
         wide = dot(dot(pick, hy[t]).astype(BF16), spread)
         my[t] = jnp.where(keep, wide, 0.0).astype(BF16)
@@ -184,25 +208,27 @@
 
     halves = 2 if n_pz % 2 == 0 and n_pz & (n_pz - 1) == 0 else 1
     half_rows = depth_y // halves
-    for f in range(fields):
+    for f, c in [(f, c) for f in range(fields) for c in range(CUTS)]:
         for o in range(n_py - 1, 0, -1):
-            copy_y(f, o).wait_recv()
-        high, low = split(lines[f])
+            copy_y(f, c, o).wait_recv()
+        high, low = split(lines[f, c])
         for h in range(halves):
             part = lax.rem(pz // (n_pz // halves) + h + 1, halves)
             span = pl.ds(pl.multiple_of(part * half_rows, half_rows), half_rows)
-            parts_out[f, span] = rows_transform(my[0, span], my[1, span], high, low)
+            parts_out[f, c, span] = rows_transform(my[0, span], my[1, span], high, low)
             top = n_pz - h * (n_pz // halves)
             for o in range(top - 1, max(top - n_pz // halves, 1) - 1, -1):
-                copy_z(f, o).start()
-        parts[f, pl.ds(pz * rows_z, rows_z)] = parts_out[f, pl.ds(pz * rows_z, rows_z)]
+                copy_z(f, c, o).start()
+        parts[f, pl.ds((pz * CUTS + c) * rows_z, rows_z)] = parts_out[
+            f, c, pl.ds(pz * rows_z, rows_z)
+        ]
 
     row, col = iota((rows_out, nz), 0), iota((rows_out, nz), 1)
     pick = (row % nz == col).astype(F32).astype(BF16)
     row, col = iota((nz, depth_z), 0), iota((nz, depth_z), 1)
-    spread = ((col // rows_z) * zl + col % zl == row).astype(F32).astype(BF16)
+    spread = ((col // rows_z) * zc + col % zc == row).astype(F32).astype(BF16)
     row, col = iota((rows_out, depth_z), 0), iota((rows_out, depth_z), 1)
-    keep = row // nz == (col // zl) % share_y
+    keep = row // nz == (col // zc) % share_y
     for t in range(2):
         wide = dot(dot(pick, hz[t]).astype(BF16), spread)
         mz[t] = jnp.where(keep, wide, 0.0).astype(BF16)
@@ -216,8 +242,9 @@
 
     last = fields - 1
     for f in range(fields):
-        for o in range(n_pz - 1, 0, -1):
-            copy_z(f, o).wait_recv()
+        for c in range(CUTS):
+            for o in range(n_pz - 1, 0, -1):
+                copy_z(f, c, o).wait_recv()
         high, low = split(parts[f])
         if f < last:
             modes[f] = rows_transform(mz[0], mz[1], high, low)
@@ -239,11 +266,11 @@
             for a in range(fields):
                 new = out_ref[a] + coupling[a, last] * rest
                 out_ref[a] = new + weight * result if a == last else new
-    for f in range(fields):
+    for f, c in [(f, c) for f in range(fields) for c in range(CUTS)]:
         for o in range(1, n_py):
-            copy_y(f, o).wait_send()
+            copy_y(f, c, o).wait_send()
         for o in range(1, n_pz):
-            copy_z(f, o).wait_send()
+            copy_z(f, c, o).wait_send()
 
 
 def shards(n_py, n_pz, species, coupling, symbol_x, symbol_y, symbol_z):
@@ -253,20 +280,22 @@
     block = fields * nx * yl * zl
     tables = 2 * (nx * nx + (ny * zl) ** 2 + (share_y * nz) ** 2)
     need = 7 * 4 * block + 2 * tables + 16 * max(ny * zl, share_y * nz) ** 2
-    if share_x % LANES or zl % SUBLANES or nx % n_py or ny % n_pz or need > VMEM_BUDGET or fields < 2:
+    fits = need <= VMEM_BUDGET and fields > 1 and zl % CUTS == 0 and nz % SUBLANES == 0
+    fits = fits and yl % SUBLANES == 0 and share_y * (zl // CUTS) % SUBLANES == 0
+    if share_x % LANES or nx % n_py or ny % n_pz or not fits:
         return plain_shards(species, coupling, symbol_x, symbol_y, symbol_z)
     dims = (fields, ny, nz, n_py, n_pz, yl, zl, share_x, share_y)
-    rows_y, depth_y, depth_z = yl * zl, ny * zl, share_y * nz
+    rows_y, depth_y, depth_z = yl * zl // CUTS, ny * zl // CUTS, share_y * nz
     vmem = pl.BlockSpec(memory_space=pltpu.VMEM)
     hbm = pl.BlockSpec(memory_space=pltpu.HBM)
-    values = jnp.transpose(species, (0, 2, 3, 1)).reshape(fields, rows_y, nx)
+    values = jnp.transpose(species, (0, 2, 3, 1)).reshape(fields, yl * zl, nx)
     out = pl.pallas_call(
         functools.partial(kernel, dims),
         out_shape=jax.ShapeDtypeStruct((fields, depth_z, share_x), F32),
         in_specs=[hbm] * 8,
         out_specs=vmem,
         scratch_shapes=[
-            pltpu.VMEM((fields, rows_y, nx), F32),
+            pltpu.VMEM((fields, nx // LANES, yl * zl, LANES), F32),
             pltpu.VMEM((2, nx, nx), BF16),
             pltpu.VMEM((2, ny, ny), BF16),
             pltpu.VMEM((2, nz, nz), BF16),
@@ -274,20 +303,20 @@
             pltpu.VMEM((1, nx), F32),
             pltpu.SMEM((ny,), F32),
             pltpu.VMEM((1, nz), F32),
-            pltpu.VMEM((fields, n_py, rows_y, share_x), F32),
-            pltpu.VMEM((fields, depth_y, share_x), F32),
-            pltpu.VMEM((fields, depth_y, share_x), F32),
+            pltpu.VMEM((fields, CUTS, n_py, rows_y, share_x), F32),
+            pltpu.VMEM((fields, CUTS, depth_y, share_x), F32),
+            pltpu.VMEM((fields, CUTS, depth_y, share_x), F32),
             pltpu.VMEM((fields, depth_z, share_x), F32),
             pltpu.VMEM((fields - 1, depth_z, share_x), F32),
             pltpu.VMEM((depth_z, share_x), F32),
             pltpu.VMEM((2, depth_y, depth_y), BF16),
             pltpu.VMEM((2, depth_z, depth_z), BF16),
-            pltpu.SemaphoreType.DMA((fields,)),
+            pltpu.SemaphoreType.DMA((fields, nx // LANES)),
             pltpu.SemaphoreType.DMA((8,)),
-            pltpu.SemaphoreType.DMA((fields, n_py)),
-            pltpu.SemaphoreType.DMA((fields, n_py)),
-            pltpu.SemaphoreType.DMA((fields, n_pz)),
-            pltpu.SemaphoreType.DMA((fields, n_pz)),
+            pltpu.SemaphoreType.DMA((fields * CUTS, n_py)),
+            pltpu.SemaphoreType.DMA((fields * CUTS, n_py)),
+            pltpu.SemaphoreType.DMA((fields * CUTS, n_pz)),
+            pltpu.SemaphoreType.DMA((fields * CUTS, n_pz)),
         ],
         compiler_params=pltpu.CompilerParams(
             collective_id=0, has_side_effects=True, vmem_limit_bytes=67043328

time: 39 us -> 39.1 us (level)
  no operation moved by 1% of the time
where the time goes in v4:
time: 39.1 us; the launch traced here: 38.9 us
  Pallas kernels  36.6 us (94%)
  local copies, waits for them, and re-layouts  2.31 us (6%)
    pallas_call x1, Pallas kernels, shards(): pl.pallas_call(functools.partial(kernel, dims), out_shape=jax.ShapeDtypeS...  36.6 us
    unnamed x1, local copies, waits for them, and re-layouts  2.31 us

profile of v4, /device:TPU:0, one launch (start us, length us, event | category | flops | bytes accessed | tf_op | source)
XLA Modules:
  0.0 38.9 jit_solution(6571352726185731452)
XLA Ops:
  0.0 36.6 %shard_map.82 = f32[4,512,128]{2,1,0:T(8,128)} custom-call(f32[4,128,512]{2,1,0:T(8,128)} %bitcast.9, bf16[2,512,512]{2,1,0:T(8,128)(2,1)} %constant.4.clone.hx_hbm, bf16[2,64,64]{2,1,0:T(8,128)(2,1)} %constant.5.clone.hy_hbm.hz_hbm, bf16[2,64,64]{2,1,0:T(8,128)(2,1)} %constant.5.clone.hy_hbm.hz_hbm, f32[4,4]{1,0:T(4,128)} %coupling_hbm.1, ...), custom_call_target="tpu_custom_call" | custom-call | tf_op jit(solution)/shard_map/pallas_call | solution.py:292
  36.6 2.3 %copy.10 = f32[4,128,8,64]{1,3,2,0:T(8,128)} copy(f32[4,128,8,64]{1,3,2,0:T(8,128)} %bitcast.8) | data formatting | bytes 2097152

commit v5 on v3

--- a/solution.py
+++ b/solution.py
@@ -290,7 +290,7 @@
             pltpu.SemaphoreType.DMA((fields, n_pz)),
         ],
         compiler_params=pltpu.CompilerParams(
-            collective_id=0, has_side_effects=True, vmem_limit_bytes=67043328
+            collective_id=0, has_side_effects=True, vmem_limit_bytes=54500000
         ),
     )(
         values,

time: 39 us -> 38.2 us (0.979)
  Pallas kernels: 36.5 us -> 35.6 us
    pallas_call x1, Pallas kernels: 36.5 us -> 35.6 us  [shards(): pl.pallas_call(functools.partial(kernel, dims), out_shape=jax.ShapeDtypeS...]
    unnamed x1 -> x11, local copies, waits for them, and re-layouts: 2.31 us -> 2.43 us
where the time goes in v5:
time: 38.2 us; the launch traced here: 38 us
  Pallas kernels  35.6 us (93%)
  local copies, waits for them, and re-layouts  2.43 us (6%)
    pallas_call x1, Pallas kernels, shards(): pl.pallas_call(functools.partial(kernel, dims), out_shape=jax.ShapeDtypeS...  35.6 us
    unnamed x11, local copies, waits for them, and re-layouts  2.43 us

profile of v5, /device:TPU:0, one launch (start us, length us, event | category | flops | bytes accessed | tf_op | source)
XLA Modules:
  0.0 38.0 jit_solution(13674102365229037284)
XLA Ops:
  0.0 0.0 copy-start.2
  0.0 0.0 copy-start.1
  0.0 0.0 copy-start.3
  0.0 0.0 copy-start.4
  0.0 0.7 %copy-done.2 = f32[512]{0:T(512)S(1)} copy-done((f32[512]{0:T(512)S(1)}, f32[512]{0:T(512)}, u32[]{:S(2)}) %copy-start.2) | copy-done | bytes 2072
  0.7 0.0 copy-done.1
  0.7 0.0 copy-done.3
  0.7 0.0 copy-done.4
  0.7 0.0 copy-start
  0.7 0.8 %copy-done = bf16[2,64,64]{2,1,0:T(8,128)(2,1)S(1)} copy-done((bf16[2,64,64]{2,1,0:T(8,128)(2,1)S(1)}, bf16[2,64,64]{2,1,0:T(8,128)(2,1)}, u32[]{:S(2)}) %copy-start) | copy-done | bytes 16408
  1.5 35.6 %shard_map.82 = f32[4,512,128]{2,1,0:T(8,128)S(1)} custom-call(f32[4,128,512]{2,1,0:T(8,128)} %bitcast.11, bf16[2,512,512]{2,1,0:T(8,128)(2,1)} %constant.4.clone.hx_hbm, bf16[2,64,64]{2,1,0:T(8,128)(2,1)S(1)} %copy-done, bf16[2,64,64]{2,1,0:T(8,128)(2,1)S(1)} %copy-done, f32[4,4]{1,0:T(4,128)S(1)} %copy-done.1, f32[1,512]{1,0:T(1,128)S(1)} %bitcast.9, ...), custom_call_target="tpu_custom_call" | custom-call | tf_op jit(solution)/shard_map/pallas_call | solution.py:263
  37.0 1.0 %copy.10 = f32[4,128,8,64]{1,3,2,0:T(8,128)} copy(f32[4,128,8,64]{1,3,2,0:T(8,128)S(1)} %bitcast.8) | data formatting | bytes 2097152
Async XLA Ops:
  0.0 0.7 %copy-start.2 = (f32[512]{0:T(512)S(1)}, f32[512]{0:T(512)}, u32[]{:S(2)}) copy-start(f32[512]{0:T(512)} %param.10) | copy-start | bytes 6148
  0.0 0.7 %copy-start.1 = (f32[4,4]{1,0:T(4,128)S(1)}, f32[4,4]{1,0:T(4,128)}, u32[]{:S(2)}) copy-start(f32[4,4]{1,0:T(4,128)} %coupling_hbm.1) | copy-start | bytes 196
  0.0 0.7 %copy-start.3 = (f32[64]{0:T(128)S(1)}, f32[64]{0:T(128)}, u32[]{:S(2)}) copy-start(f32[64]{0:T(128)} %sy_hbm.1) | copy-start | bytes 772
  0.0 0.7 %copy-start.4 = (f32[64]{0:T(128)S(1)}, f32[64]{0:T(128)}, u32[]{:S(2)}) copy-start(f32[64]{0:T(128)} %param.12) | copy-start | bytes 772
  0.7 0.8 %copy-start = (bf16[2,64,64]{2,1,0:T(8,128)(2,1)S(1)}, bf16[2,64,64]{2,1,0:T(8,128)(2,1)}, u32[]{:S(2)}) copy-start(bf16[2,64,64]{2,1,0:T(8,128)(2,1)} %constant.5.clone.hy_hbm.hz_hbm) | copy-start | bytes 49156
